TPU v7x, 32 devices: a whole 2x2x4 slice. The times are simulated.
32 devices in a mesh: shot: 4 (over y, core), tile: 8 (over z, x).
Axes of the slice: x: 2, y: 2, z: 4, core: 2. Of those that a mesh axis runs over, the one named last changes fastest.
Arguments:
- source: bfloat16 [64, 1, 32, 32, 128], P(('shot', 'tile')), may hold values from -6 to 6
- receiver: bfloat16 [64, 1, 32, 32, 128], P(('shot', 'tile')), may hold values from -6 to 6
- corners: int32 [64, 2], P(('shot', 'tile')), may hold values from 0 to 224, as said below
Outputs:
- filtered: float32 [32, 256, 256], P('tile', 'shot')
Inputs may be any that keep to these rules, and one draw needn't show every extreme that they name: corners[s, 0] is at most 224 and corners[s, 1] at most 128, so every box lies inside the image.
All inputs are finite; a program needn't handle non-finite values.
Results may differ from a plain program's by a relative error of at most 0.0003.
Values may be sent and summed in bfloat16 or wider, within the bound.
A program may use at most 64 MiB of HBM per device.

v0:
```python
import jax
import jax.numpy as jnp
from jax import lax
from jax.sharding import PartitionSpec as P

X = 256
Y = 256


damping = 1.0


def with_halo(cells, sides, width):
    for axis, dim in sides:
        count = lax.axis_size(axis)
        ends = count - 1
        head = lax.slice_in_dim(cells, 0, width, axis=dim)
        tail = lax.slice_in_dim(cells, cells.shape[dim] - width, cells.shape[dim], axis=dim)
        cells = jnp.concatenate(
            [
                lax.ppermute(tail, axis, [(i, (i + 1) % count) for i in range(ends)]),
                cells,
                lax.ppermute(head, axis, [((i + 1) % count, i) for i in range(ends)]),
            ],
            axis=dim,
        )
    return cells


def laplace(padded):
    center = padded[1:-1, 1:-1, 1:-1]
    beside = padded[2:, 1:-1, 1:-1] + padded[:-2, 1:-1, 1:-1]
    beside = beside + padded[1:-1, 2:, 1:-1] + padded[1:-1, :-2, 1:-1]
    beside = beside + padded[1:-1, 1:-1, 2:] + padded[1:-1, 1:-1, :-2]
    return beside - 6.0 * center


def correlate(wave_bf, back_bf, time_axis):
    wave = wave_bf.astype(jnp.float32)
    back = back_bf.astype(jnp.float32)
    return jnp.stack((jnp.sum(wave * back, axis=time_axis), jnp.sum(wave * wave, axis=time_axis)))


def per_device(source, receiver, corners):
    tile_count = lax.axis_size("tile")
    slab_depth = source.shape[2] // tile_count
    box_rows = source.shape[3]
    box_cols = source.shape[4]
    got_wave, got_back = (
        lax.all_to_all(source, "tile", split_axis=2, concat_axis=0, tiled=True),
        lax.all_to_all(receiver, "tile", split_axis=2, concat_axis=0, tiled=True),
    )
    stacked = correlate(got_wave, got_back, 1)
    corner_all = lax.all_gather(corners, "tile", axis=0, tiled=True)
    col_index = jnp.arange(Y, dtype=jnp.int32)
    box_col = jnp.arange(box_cols, dtype=jnp.int32)
    col_table = (
        col_index[None, None, :] == corner_all[:, 1][:, None, None] + box_col[None, :, None]
    ).astype(jnp.float32)
    placed = jnp.einsum("qkzab,kby->qzkay", stacked, col_table, precision=lax.Precision.HIGHEST)
    shots_in = corner_all.shape[0]
    placed = placed.reshape(2, slab_depth, shots_in * box_rows, Y)
    row_target = (
        corner_all[:, 0][:, None] + jnp.arange(box_rows, dtype=jnp.int32)[None, :]
    ).reshape(-1)
    row_index = jnp.arange(X, dtype=jnp.int32)
    row_table = (row_target[:, None] == row_index[None, :]).astype(jnp.float32)
    sums = jnp.einsum("rx,qzry->qzxy", row_table, placed, precision=lax.Precision.HIGHEST)
    image_part = sums[0]
    light_part = sums[1]
    image_sum, light_sum = (
        lax.psum_scatter(image_part, "shot", scatter_dimension=1, tiled=True),
        lax.psum_scatter(light_part, "shot", scatter_dimension=1, tiled=True),
    )
    normal = image_sum / (damping + light_sum)
    padded = with_halo(normal, (("shot", 1), ("tile", 0)), 1)
    padded = jnp.pad(padded, ((0, 0), (0, 0), (1, 1)))
    return laplace(padded)


def solution(mesh):
    return jax.shard_map(
        per_device,
        mesh=mesh,
        in_specs=(
            P(("shot", "tile"), None, None, None, None),
            P(("shot", "tile"), None, None, None, None),
            P(("shot", "tile"), None),
        ),
        out_specs=P("tile", "shot", None),
        check_vma=False,
    )
```

profile of v0, /device:TPU:1, one launch (start us, length us, event | category | flops | bytes accessed | tf_op | source)
XLA Modules:
  0.0 143.0 jit_solution(10602599561009317554)
XLA Ops:
  6.5 2.0 %copy.15 = bf16[2,1,32,32,128]{4,3,1,0,2:T(8,128)(2,1)} copy(bf16[2,1,32,32,128]{4,3,2,1,0:T(8,128)(2,1)} %param.3) | data formatting | bytes 1048576 | tf_op args[0]
  8.5 6.3 %all-to-all-start = ((bf16[2,1,32,32,128]{4,3,1,0,2:T(8,128)(2,1)}), bf16[2,1,32,32,128]{4,3,1,0,2:T(8,128)(2,1)S(1)}, u32[]{:S(2)}, u32[]{:S(2)}) async-start(bf16[2,1,32,32,128]{4,3,1,0,2:T(8,128)(2,1)} %copy.15), calls=%async_computation | async-start | bytes 1048576 | tf_op jit(solution)/shard_map/all_to_all | solution.py:50
  14.9 0.9 copy.16
  15.7 12.5 %all-to-all-done = bf16[2,1,32,32,128]{4,3,1,0,2:T(8,128)(2,1)S(1)} async-done(((bf16[2,1,32,32,128]{4,3,1,0,2:T(8,128)(2,1)}), bf16[2,1,32,32,128]{4,3,1,0,2:T(8,128)(2,1)S(1)}, u32[]{:S(2)}, u32[]{:S(2)}) %all-to-all-start) | async-done | bytes 524320 | tf_op jit(solution)/shard_map/all_to_all | solution.py:50
  28.3 4.9 %all-to-all-start.1 = ((bf16[2,1,32,32,128]{4,3,1,0,2:T(8,128)(2,1)}), bf16[2,1,32,32,128]{4,3,1,0,2:T(8,128)(2,1)S(1)}, u32[]{:S(2)}, u32[]{:S(2)}) async-start(bf16[2,1,32,32,128]{4,3,1,0,2:T(8,128)(2,1)} %copy.16), calls=%async_computation.1 | async-start | bytes 1048576 | tf_op jit(solution)/shard_map/all_to_all | solution.py:51
  33.2 19.8 %all-gather = s32[8,2,2]{2,1,0:T(2,128)S(1)} all-gather(s32[1,2,2]{2,1,0:T(2,128)S(1)} %bitcast.41), channel_id=1, replica_groups=mesh['shot'=4,'tile'=8] {'tile'}, dimensions={0}, use_global_device_ids=true | all-gather | bytes 144 | tf_op jit(solution)/shard_map/all_gather | solution.py:54
  53.0 0.1 fusion.17
  53.1 0.1 copy.29
  53.2 0.1 copy.28
  53.3 0.1 add.74
  53.4 0.1 iota_add_fusion.1
  53.5 0.3 convert_multiply_fusion.1
  53.8 0.1 copy.17
  54.0 2.3 %convolution_bitcast_fusion = f32[2,4,16,32,256]{4,3,1,0,2:T(8,128)S(1)} fusion(f32[1,16,4,32,128]{4,3,2,0,1:T(8,128)S(1)} %bitcast.37, f32[1,16,4,32,128]{4,3,2,0,1:T(8,128)S(1)} %bitcast.36, s32[16,128]{1,0:T(8,128)S(1)} %iota_add_fusion.1), kind=kOutput, calls=%fused_computation | convolution fusion | flops 1611661312 | bytes 6299648 | tf_op jit(solution)/shard_map/qkzab,kby->qzkay/dot_general | solution.py:60
  56.2 0.6 copy.19
  56.8 3.6 %convolution_bitcast_fusion.1 = f32[2,4,256,256]{2,3,1,0:T(8,128)S(1)} fusion(f32[2,4,512,256]{3,2,1,0:T(8,128)S(1)} %bitcast.33, s32[512]{0:T(512)S(1)} %add.74), kind=kOutput, calls=%fused_computation.6 | convolution fusion | flops 3221356544 | bytes 6293504 | tf_op jit(solution)/shard_map/rx,qzry->qzxy/dot_general | solution.py:68
  60.5 0.2 slice_bitcast_fusion.1
  60.7 1.3 copy.21
  62.0 1.3 copy.22
  63.4 0.6 dynamic-slice
  64.6 52.2 %all-reduce.6.cloned.1.call-done = (f32[4,256,256]{2,0,1:T(4,128)}, f32[4,256,256]{2,0,1:T(4,128)}) async-done(((f32[4,256,256]{2,0,1:T(4,128)}, f32[4,256,256]{2,0,1:T(4,128)}), (f32[4,256,256]{2,0,1:T(4,128)}, f32[4,256,256]{2,0,1:T(4,128)})) %all-reduce.6.cloned.1.call-update) | async-done | bytes 2097168
  116.8 1.1 fusion.13
  118.0 2.8 %collective-permute-start = (f32[4,1,256]{2,0,1:T(4,128)S(1)}, f32[4,1,256]{2,0,1:T(4,128)S(1)}, u32[]{:S(2)}, u32[]{:S(2)}) collective-permute-start(f32[4,1,256]{2,0,1:T(4,128)S(1)} %get-tuple-element.13), channel_id=1, source_target_pairs={{0,8},{8,16},{16,24},{1,9},{9,17},{17,25},{2,10},{10,18},{18,26},{... | collective-permute-start | bytes 12296 | tf_op jit(solution)/shard_map/ppermute | solution.py:21
  120.8 1.9 %collective-permute-start.1 = (f32[4,1,256]{2,0,1:T(4,128)S(1)}, f32[4,1,256]{2,0,1:T(4,128)S(1)}, u32[]{:S(2)}, u32[]{:S(2)}) collective-permute-start(f32[4,1,256]{2,0,1:T(4,128)S(1)} %get-tuple-element.14), channel_id=1, source_target_pairs={{8,0},{16,8},{24,16},{9,1},{17,9},{25,17},{10,2},{18,10},{26,18},{... | collective-permute-start | bytes 12296 | tf_op jit(solution)/shard_map/ppermute | solution.py:23
  122.7 3.0 %collective-permute-done.1 = f32[4,1,256]{2,0,1:T(4,128)S(1)} collective-permute-done((f32[4,1,256]{2,0,1:T(4,128)S(1)}, f32[4,1,256]{2,0,1:T(4,128)S(1)}, u32[]{:S(2)}, u32[]{:S(2)}) %collective-permute-start.1) | collective-permute-done | bytes 4128 | tf_op jit(solution)/shard_map/ppermute | solution.py:23
  125.7 0.1 pad_maximum_fusion.8
  125.8 3.3 %collective-permute-start.3 = (f32[1,66,256]{2,0,1:T(1,128)S(1)}, f32[1,66,256]{2,0,1:T(1,128)S(1)}, u32[]{:S(2)}, u32[]{:S(2)}) collective-permute-start(f32[1,66,256]{2,0,1:T(1,128)S(1)} %get-tuple-element.11), channel_id=1, source_target_pairs={{0,1},{1,2},{2,3},{3,4},{4,5},{5,6},{6,7},{8,9},{9,10},{10,11},{11... | collective-permute-start | bytes 202760 | tf_op jit(solution)/shard_map/ppermute | solution.py:21
  129.2 1.3 collective-permute-start.2
  130.5 3.7 %collective-permute-done.2 = f32[1,66,256]{2,0,1:T(1,128)S(1)} collective-permute-done((f32[1,66,256]{2,0,1:T(1,128)S(1)}, f32[1,66,256]{2,0,1:T(1,128)S(1)}, u32[]{:S(2)}, u32[]{:S(2)}) %collective-permute-start.2) | collective-permute-done | bytes 67616 | tf_op jit(solution)/shard_map/ppermute | solution.py:23
  134.2 0.7 select_maximum_fusion
  134.9 0.5 fusion.9
  135.4 0.8 copy.23
  (14 shorter events, 0.2 us)
Async XLA Ops:
  6.5 8.3 %copy-start = (bf16[2,1,32,32,128]{4,3,2,1,0:T(8,128)(2,1)S(1)}, bf16[2,1,32,32,128]{4,3,2,1,0:T(8,128)(2,1)}, u32[]{:S(2)}) copy-start(bf16[2,1,32,32,128]{4,3,2,1,0:T(8,128)(2,1)} %param.4) | copy-start | bytes 1572868
  6.5 26.7 %copy-start.1 = (s32[2,2]{1,0:T(2,128)S(1)}, s32[2,2]{1,0:T(2,128)}, u32[]{:S(2)}) copy-start(s32[2,2]{1,0:T(2,128)} %param.5) | copy-start | bytes 52
  8.5 19.8 %all-to-all-start = ((bf16[2,1,32,32,128]{4,3,1,0,2:T(8,128)(2,1)}), bf16[2,1,32,32,128]{4,3,1,0,2:T(8,128)(2,1)S(1)}, u32[]{:S(2)}, u32[]{:S(2)}) async-start(bf16[2,1,32,32,128]{4,3,1,0,2:T(8,128)(2,1)} %copy.15), calls=%async_computation | async-start | bytes 1048576 | tf_op jit(solution)/shard_map/all_to_all | solution.py:50
  28.3 25.2 %all-to-all-start.1 = ((bf16[2,1,32,32,128]{4,3,1,0,2:T(8,128)(2,1)}), bf16[2,1,32,32,128]{4,3,1,0,2:T(8,128)(2,1)S(1)}, u32[]{:S(2)}, u32[]{:S(2)}) async-start(bf16[2,1,32,32,128]{4,3,1,0,2:T(8,128)(2,1)} %copy.16), calls=%async_computation.1 | async-start | bytes 1048576 | tf_op jit(solution)/shard_map/all_to_all | solution.py:51
  33.2 83.7 %all-reduce.6.cloned.1.call-start = ((), (), s32[]{:S(2)}) async-start(), calls=%async_computation.2 | async-start | bytes 4194304
  62.0 1.3 copy-start.2
  118.0 4.8 %collective-permute-start = (f32[4,1,256]{2,0,1:T(4,128)S(1)}, f32[4,1,256]{2,0,1:T(4,128)S(1)}, u32[]{:S(2)}, u32[]{:S(2)}) collective-permute-start(f32[4,1,256]{2,0,1:T(4,128)S(1)} %get-tuple-element.13), channel_id=1, source_target_pairs={{0,8},{8,16},{16,24},{1,9},{9,17},{17,25},{2,10},{10,18},{18,26},{... | collective-permute-start | bytes 12296 | tf_op jit(solution)/shard_map/ppermute | solution.py:21
  120.8 4.9 %collective-permute-start.1 = (f32[4,1,256]{2,0,1:T(4,128)S(1)}, f32[4,1,256]{2,0,1:T(4,128)S(1)}, u32[]{:S(2)}, u32[]{:S(2)}) collective-permute-start(f32[4,1,256]{2,0,1:T(4,128)S(1)} %get-tuple-element.14), channel_id=1, source_target_pairs={{8,0},{16,8},{24,16},{9,1},{17,9},{25,17},{10,2},{18,10},{26,18},{... | collective-permute-start | bytes 12296 | tf_op jit(solution)/shard_map/ppermute | solution.py:23
  125.8 4.6 %collective-permute-start.3 = (f32[1,66,256]{2,0,1:T(1,128)S(1)}, f32[1,66,256]{2,0,1:T(1,128)S(1)}, u32[]{:S(2)}, u32[]{:S(2)}) collective-permute-start(f32[1,66,256]{2,0,1:T(1,128)S(1)} %get-tuple-element.11), channel_id=1, source_target_pairs={{0,1},{1,2},{2,3},{3,4},{4,5},{5,6},{6,7},{8,9},{9,10},{10,11},{11... | collective-permute-start | bytes 202760 | tf_op jit(solution)/shard_map/ppermute | solution.py:21
  129.2 5.0 %collective-permute-start.2 = (f32[1,66,256]{2,0,1:T(1,128)S(1)}, f32[1,66,256]{2,0,1:T(1,128)S(1)}, u32[]{:S(2)}, u32[]{:S(2)}) collective-permute-start(f32[1,66,256]{2,0,1:T(1,128)S(1)} %get-tuple-element.12), channel_id=1, source_target_pairs={{1,0},{2,1},{3,2},{4,3},{5,4},{6,5},{7,6},{9,8},{10,9},{11,10},{12... | collective-permute-start | bytes 202760 | tf_op jit(solution)/shard_map/ppermute | solution.py:23
Sparse Core Ops, SparseCore 0:
  63.5 53.2 all-reduce.5
where the time goes:
time: 143 us
  waiting for transfers between devices  71.5 us (50%)
  starting transfers between devices  20.6 us (14%)
  blocking collectives  19.8 us (14%)
  between operations  14.2 us (10%)
  local copies, waits for them, and re-layouts  8.1 us (6%)
  matrix products  5.91 us (4%)
  other arithmetic  2.88 us (2%)
    unnamed x2, waiting for transfers between devices  52.2 us
    all_gather x1, blocking collectives, per_device(): corner_all = lax.all_gather(corners, 'tile', axis=0, tiled=True)  19.8 us
    all_to_all x1, waiting for transfers between devices, per_device(): lax.all_to_all(source, 'tile', split_axis=2, concat_axis=0, tiled=True)  12.5 us
    ppermute x2, waiting for transfers between devices, with_halo(): lax.ppermute(head, axis, [((i + 1) % count, i) for i in range(ends)])  6.69 us
    all_to_all x1, starting transfers between devices, per_device(): lax.all_to_all(source, 'tile', split_axis=2, concat_axis=0, tiled=True)  6.34 us
    ppermute x2, starting transfers between devices, with_halo(): lax.ppermute(tail, axis, [(i, (i + 1) % count) for i in range(ends)])  6.15 us
    all_to_all x1, starting transfers between devices, per_device(): lax.all_to_all(receiver, 'tile', split_axis=2, concat_axis=0, tiled=True)  4.88 us
    dot_general x1, matrix products, per_device(): jnp.einsum('rx,qzry->qzxy', row_table, placed, precision=lax.Precision.HI...  3.63 us
  transfers between devices with their start and end apart: 7, of which 4 were waited for; matrix products, arithmetic and copies ran while one was open for 1% of the time, Pallas kernels for 0%

commit v1 on v0

v1 whole, which is shorter than its diff:
```python
import functools

import jax
import jax.numpy as jnp
from jax import lax
from jax.experimental import pallas as pl
from jax.experimental.pallas import tpu as pltpu
from jax.sharding import PartitionSpec as P

X = 256
Y = 256
LANES = 128

damping = 1.0


def kernel(
    ns, nt, src, rcv, cor, out, rx, cbuf, csm, boxes, acc, r1, r2, nrm, hx, hz, rows,
    rx_send, rx_recv, c_send, c_recv, c_local, s1_send, s1_recv, s2_send, s2_recv, h_send, h_recv,
):
    depth, strip, width = nrm.shape
    spd, samples = src.shape[0], src.shape[1]
    box_rows = src.shape[3]
    halves = width // LANES
    shots = nt * spd
    block = min(box_rows, strip)
    per_strip = strip // block
    half_ns = ns // 2
    shot = lax.axis_index("shot")
    tile = lax.axis_index("tile")
    core = lax.rem(shot, 2)
    pair = shot // 2
    other = 1 - core

    barrier = pltpu.get_barrier_semaphore()
    for k in range(1, ns):
        pl.semaphore_signal(barrier, inc=1, device_id={"shot": lax.rem(shot + k, ns)})
    for k in range(1, nt):
        pl.semaphore_signal(barrier, inc=1, device_id={"tile": lax.rem(tile + k, nt)})

    own = []
    for p in range(depth):
        for w, ref in enumerate((src, rcv)):
            copy = pltpu.make_async_copy(ref.at[:, :, tile * depth + p], rx.at[p, tile, w], rx_recv.at[p])
            copy.start()
    own_corner = pltpu.make_async_copy(cor, cbuf.at[tile], c_recv)
    own_corner.start()

    pl.semaphore_wait(barrier, ns - 1 + nt - 1)

    for k in range(1, nt):
        to = lax.rem(tile + k, nt)
        pltpu.make_async_remote_copy(
            src_ref=cor, dst_ref=cbuf.at[tile], send_sem=c_send, recv_sem=c_recv, device_id={"tile": to}
        ).start()
    for p in range(depth):
        for k in range(1, nt):
            to = lax.rem(tile + k, nt)
            for w, ref in enumerate((src, rcv)):
                pltpu.make_async_remote_copy(
                    src_ref=ref.at[:, :, to * depth + p],
                    dst_ref=rx.at[p, tile, w],
                    send_sem=rx_send.at[p],
                    recv_sem=rx_recv.at[p],
                    device_id={"tile": to},
                ).start()

    zero = jnp.zeros((block, LANES), jnp.float32)

    def clear(s, carry):
        for q in range(2):
            for h in range(halves):
                boxes[s, q, h, pl.ds(0, block), :] = zero
                boxes[s, q, h, pl.ds(block + box_rows, block), :] = zero
        return carry

    lax.fori_loop(0, shots, clear, 0)

    pltpu.make_async_copy(cbuf, cbuf, c_recv).wait()
    to_scalar = pltpu.make_async_copy(cbuf, csm, c_local)
    to_scalar.start()
    to_scalar.wait()

    lane = lax.broadcasted_iota(jnp.int32, (box_rows, LANES), 1)

    def expand(p):
        def peer(t, carry):
            for i in range(spd):
                s = t * spd + i
                col = csm[t, i, 1]
                turn = lax.rem(col, LANES)
                image = jnp.zeros((box_rows, LANES), jnp.float32)
                light = image
                for n in range(samples):
                    wave = rx[p, t, 0, i, n].astype(jnp.float32)
                    back = rx[p, t, 1, i, n].astype(jnp.float32)
                    image = wave * back if n == 0 else image + wave * back
                    light = wave * wave if n == 0 else light + wave * wave
                image = pltpu.roll(image, turn, 1)
                light = pltpu.roll(light, turn, 1)
                for h in range(halves):
                    at = lane + (h * LANES - col)
                    inside = (at >= 0) & (at < LANES)
                    boxes[s, 0, h, pl.ds(block, box_rows), :] = jnp.where(inside, image, 0.0)
                    boxes[s, 1, h, pl.ds(block, box_rows), :] = jnp.where(inside, light, 0.0)
            return carry

        lax.fori_loop(0, nt, peer, 0)

    def place(p, parity):
        def one(n, carry):
            j = 2 * (n // per_strip) + parity
            base = lax.rem(n, per_strip) * block
            first = j * strip + base + block
            total = [[None] * halves for _ in range(2)]
            for s in range(shots):
                start = jnp.clip(first - csm[s // spd, s % spd, 0], 0, box_rows + block)
                for q in range(2):
                    for h in range(halves):
                        piece = boxes[s, q, h, pl.ds(start, block), :]
                        total[q][h] = piece if s == 0 else total[q][h] + piece
            for q in range(2):
                for h in range(halves):
                    acc[p, j, q, pl.ds(base, block), pl.ds(h * LANES, LANES)] = total[q][h]
            return carry

        lax.fori_loop(0, half_ns * per_strip, one, 0)

    def stage1(p):
        for i in range(half_ns):
            pltpu.make_async_remote_copy(
                src_ref=acc.at[p, 2 * i + other],
                dst_ref=r1.at[p, i],
                send_sem=s1_send.at[p],
                recv_sem=s1_recv.at[p],
                device_id={"shot": 2 * pair + other},
            ).start()

    def stage2(p):
        pltpu.make_async_copy(r1.at[p], r1.at[p], s1_recv.at[p]).wait()
        for k in range(1, half_ns):
            to = lax.rem(pair + k, half_ns)
            j = 2 * to + core
            acc[p, j] = acc[p, j] + r1[p, to]
            pltpu.make_async_remote_copy(
                src_ref=acc.at[p, j],
                dst_ref=r2.at[p, k - 1],
                send_sem=s2_send.at[p],
                recv_sem=s2_recv.at[p],
                device_id={"shot": j},
            ).start()

    def finish(p):
        pltpu.make_async_copy(r2.at[p], r2.at[p], s2_recv.at[p]).wait()
        image = acc[p, shot, 0] + r1[p, pair, 0]
        light = acc[p, shot, 1] + r1[p, pair, 1]
        for k in range(half_ns - 1):
            image = image + r2[p, k, 0]
            light = light + r2[p, k, 1]
        normal = image / (damping + light)
        nrm[p] = normal
        rows[0, pl.ds(p, 1), :] = normal[strip - 1 :, :]
        rows[1, pl.ds(p, 1), :] = normal[:1, :]

    for p in range(depth):
        pltpu.make_async_copy(rx.at[p], rx.at[p], rx_recv.at[p]).wait()
        expand(p)
        place(p, other)
        stage1(p)
        place(p, core)
        if p >= 1:
            stage2(p - 1)
        if p >= 2:
            finish(p - 2)
    stage2(depth - 1)
    if depth >= 2:
        finish(depth - 2)
    finish(depth - 1)

    halos = (
        (shot < ns - 1, shot > 0, {"shot": lax.rem(shot + 1, ns)}, rows.at[0], hx.at[0], 0),
        (shot > 0, shot < ns - 1, {"shot": lax.rem(shot + ns - 1, ns)}, rows.at[1], hx.at[1], 1),
        (tile < nt - 1, tile > 0, {"tile": lax.rem(tile + 1, nt)}, nrm.at[depth - 1], hz.at[0], 2),
        (tile > 0, tile < nt - 1, {"tile": lax.rem(tile + nt - 1, nt)}, nrm.at[0], hz.at[1], 3),
    )

    def halo_copy(item):
        return pltpu.make_async_remote_copy(
            src_ref=item[3], dst_ref=item[4], send_sem=h_send.at[item[5]], recv_sem=h_recv.at[item[5]], device_id=item[2]
        )

    for item in halos:
        @pl.when(item[0])
        def _(item=item):
            halo_copy(item).start()

        @pl.when(jnp.logical_not(item[1]))
        def _(item=item):
            item[4][...] = jnp.zeros(item[4].shape, jnp.float32)

    for item in halos:
        @pl.when(item[1])
        def _(item=item):
            halo_copy(item).wait_recv()

    row = lax.broadcasted_iota(jnp.int32, (strip, width), 0)
    column = lax.broadcasted_iota(jnp.int32, (strip, width), 1)
    for p in range(depth):
        center = nrm[p]
        above = nrm[p - 1] if p > 0 else hz[0]
        below = nrm[p + 1] if p < depth - 1 else hz[1]
        beside = above + below
        before = jnp.where(row == 0, hx[0, pl.ds(p, 1), :], pltpu.roll(center, 1, 0))
        after = jnp.where(row == strip - 1, hx[1, pl.ds(p, 1), :], pltpu.roll(center, strip - 1, 0))
        beside = beside + before + after
        left = jnp.where(column == 0, 0.0, pltpu.roll(center, 1, 1))
        right = jnp.where(column == width - 1, 0.0, pltpu.roll(center, width - 1, 1))
        beside = beside + left + right
        out[p] = beside - 6.0 * center

    for item in halos:
        @pl.when(item[0])
        def _(item=item):
            halo_copy(item).wait_send()

    sent = cbuf.at[pl.ds(0, nt - 1)]
    pltpu.make_async_copy(sent, sent, c_send).wait()
    for p in range(depth):
        sent = rx.at[p, pl.ds(0, nt - 1)]
        pltpu.make_async_copy(sent, sent, rx_send.at[p]).wait()
        pltpu.make_async_copy(r1.at[p], r1.at[p], s1_send.at[p]).wait()
        pltpu.make_async_copy(r2.at[p], r2.at[p], s2_send.at[p]).wait()


def solution(mesh):
    ns, nt = mesh.shape["shot"], mesh.shape["tile"]

    def step(source, receiver, corners):
        spd, samples, full_depth, box_rows, box_cols = source.shape
        depth = full_depth // nt
        strip = X // ns
        block = min(box_rows, strip)
        half_ns = ns // 2
        vmem = pltpu.VMEM
        dma = pltpu.SemaphoreType.DMA
        f32 = jnp.float32
        return pl.pallas_call(
            functools.partial(kernel, ns, nt),
            out_shape=jax.ShapeDtypeStruct((depth, strip, Y), f32),
            in_specs=[pl.BlockSpec(memory_space=pl.ANY)] * 3,
            out_specs=pl.BlockSpec(memory_space=pltpu.VMEM),
            scratch_shapes=[
                vmem((depth, nt, 2, spd, samples, box_rows, box_cols), jnp.bfloat16),
                vmem((nt, spd, 2), jnp.int32),
                pltpu.SMEM((nt, spd, 2), jnp.int32),
                vmem((nt * spd, 2, Y // LANES, box_rows + 2 * block, LANES), f32),
                vmem((depth, ns, 2, strip, Y), f32),
                vmem((depth, half_ns, 2, strip, Y), f32),
                vmem((depth, half_ns - 1, 2, strip, Y), f32),
                vmem((depth, strip, Y), f32),
                vmem((2, depth, Y), f32),
                vmem((2, strip, Y), f32),
                vmem((2, depth, Y), f32),
                dma((depth,)),
                dma((depth,)),
                dma,
                dma,
                dma,
                dma((depth,)),
                dma((depth,)),
                dma((depth,)),
                dma((depth,)),
                dma((4,)),
                dma((4,)),
            ],
            compiler_params=pltpu.CompilerParams(
                collective_id=0, has_side_effects=True, vmem_limit_bytes=60 * 1024 * 1024
            ),
        )(source, receiver, corners)

    return jax.shard_map(
        step,
        mesh=mesh,
        in_specs=(
            P(("shot", "tile"), None, None, None, None),
            P(("shot", "tile"), None, None, None, None),
            P(("shot", "tile"), None),
        ),
        out_specs=P("tile", "shot", None),
        check_vma=False,
    )
```

time: 143 us -> 44.7 us (0.31)
  the two profiles are of different devices: /device:TPU:1 before, /device:TPU:0 now
where the time goes in v1:
time: 44.7 us; the launch traced here: 44.6 us
  Pallas kernels  42.9 us (96%)
  local copies, waits for them, and re-layouts  1.67 us (4%)
    pallas_call x1, Pallas kernels, step(): pl.pallas_call(functools.partial(kernel, ns, nt), out_shape=jax.ShapeDtyp...  42.9 us
    unnamed x1, local copies, waits for them, and re-layouts  1.67 us

profile of v1, /device:TPU:0, one launch (start us, length us, event | category | flops | bytes accessed | tf_op | source)
XLA Modules:
  0.0 44.6 jit_solution(10256259765842362947)
XLA Ops:
  0.0 42.9 %shard_map.37 = f32[4,64,256]{2,1,0:T(8,128)} custom-call(bf16[2,1,32,32,128]{4,3,2,1,0:T(8,128)(2,1)} %src.1, bf16[2,1,32,32,128]{4,3,2,1,0:T(8,128)(2,1)} %rcv.1, s32[2,2]{1,0:T(2,128)} %cor.1), custom_call_target="tpu_custom_call" | custom-call | tf_op jit(solution)/shard_map/pallas_call | solution.py:247
  42.9 1.7 %copy.5 = f32[4,64,256]{2,1,0:T(8,128)} copy(f32[4,64,256]{2,1,0:T(8,128)} %shard_map.37) | data formatting | bytes 524288

commit v2 on v1

--- a/solution.py
+++ b/solution.py
@@ -14,14 +14,34 @@
 damping = 1.0
 
 
+def partner(index, k, count):
+    if count & (count - 1):
+        return lax.rem(index + k, count)
+    bit = 1
+    result = index
+    while bit < count:
+        if k & bit:
+            result = result + bit * (1 - 2 * lax.rem(index // bit, 2))
+        bit *= 2
+    return result
+
+
+def plane_order(depth):
+    if depth < 3:
+        return list(range(depth))
+    return [0, depth - 1] + list(range(1, depth - 1))
+
+
 def kernel(
-    ns, nt, src, rcv, cor, out, rx, cbuf, csm, boxes, acc, r1, r2, nrm, hx, hz, rows,
-    rx_send, rx_recv, c_send, c_recv, c_local, s1_send, s1_recv, s2_send, s2_recv, h_send, h_recv,
+    ns, nt, src, rcv, cor, out, sbuf, rx, cbuf, csm, boxes, acc, r1, r2, nrm, hx, hz, rows, lap,
+    in_sem, out_sem, rx_send, rx_recv, c_send, c_recv, c_local,
+    s1_send, s1_recv, s2_send, s2_recv, row_send, row_recv, face_send, face_recv,
 ):
     depth, strip, width = nrm.shape
     spd, samples = src.shape[0], src.shape[1]
     box_rows = src.shape[3]
     halves = width // LANES
+    order = plane_order(depth)
     shots = nt * spd
     block = min(box_rows, strip)
     per_strip = strip // block
@@ -38,32 +58,61 @@
     for k in range(1, nt):
         pl.semaphore_signal(barrier, inc=1, device_id={"tile": lax.rem(tile + k, nt)})
 
-    own = []
-    for p in range(depth):
+    for w, ref in enumerate((src, rcv)):
+        for i in range(spd):
+            for n in range(samples):
+                pltpu.make_async_copy(ref.at[i, n], sbuf.at[:, w, i, n], in_sem).start()
+    pltpu.make_async_copy(cor, cbuf.at[tile], c_recv).start()
+    for p in order:
         for w, ref in enumerate((src, rcv)):
-            copy = pltpu.make_async_copy(ref.at[:, :, tile * depth + p], rx.at[p, tile, w], rx_recv.at[p])
-            copy.start()
-    own_corner = pltpu.make_async_copy(cor, cbuf.at[tile], c_recv)
-    own_corner.start()
+            pltpu.make_async_copy(ref.at[:, :, tile * depth + p], rx.at[p, tile, w], rx_recv.at[p]).start()
+    pltpu.make_async_copy(sbuf, sbuf, in_sem).wait()
 
     pl.semaphore_wait(barrier, ns - 1 + nt - 1)
 
-    for k in range(1, nt):
-        to = lax.rem(tile + k, nt)
-        pltpu.make_async_remote_copy(
-            src_ref=cor, dst_ref=cbuf.at[tile], send_sem=c_send, recv_sem=c_recv, device_id={"tile": to}
-        ).start()
-    for p in range(depth):
-        for k in range(1, nt):
-            to = lax.rem(tile + k, nt)
-            for w, ref in enumerate((src, rcv)):
+    for p in order:
+        for k in range(nt - 1, 0, -1):
+            to = partner(tile, k, nt)
+            if p == order[0]:
                 pltpu.make_async_remote_copy(
-                    src_ref=ref.at[:, :, to * depth + p],
-                    dst_ref=rx.at[p, tile, w],
-                    send_sem=rx_send.at[p],
-                    recv_sem=rx_recv.at[p],
-                    device_id={"tile": to},
+                    src_ref=cor, dst_ref=cbuf.at[tile], send_sem=c_send, recv_sem=c_recv, device_id={"tile": to}
                 ).start()
+            pltpu.make_async_remote_copy(
+                src_ref=sbuf.at[to * depth + p],
+                dst_ref=rx.at[p, tile],
+                send_sem=rx_send.at[p],
+                recv_sem=rx_recv.at[p],
+                device_id={"tile": to},
+            ).start()
+
+    edges = (
+        (shot < ns - 1, shot > 0, {"shot": lax.rem(shot + 1, ns)}),
+        (shot > 0, shot < ns - 1, {"shot": lax.rem(shot + ns - 1, ns)}),
+    )
+    faces = (
+        (tile < nt - 1, tile > 0, {"tile": lax.rem(tile + 1, nt)}, depth - 1),
+        (tile > 0, tile < nt - 1, {"tile": lax.rem(tile + nt - 1, nt)}, 0),
+    )
+    for d in range(2):
+        @pl.when(jnp.logical_not(edges[d][1]))
+        def _(d=d):
+            hx[d] = jnp.zeros((depth, 1, width), jnp.float32)
+
+        @pl.when(jnp.logical_not(faces[d][1]))
+        def _(d=d):
+            hz[d] = jnp.zeros((strip, width), jnp.float32)
+
+    def edge_copy(d, p):
+        return pltpu.make_async_remote_copy(
+            src_ref=rows.at[d, p], dst_ref=hx.at[d, p],
+            send_sem=row_send.at[d, p], recv_sem=row_recv.at[d, p], device_id=edges[d][2],
+        )
+
+    def face_copy(d):
+        return pltpu.make_async_remote_copy(
+            src_ref=nrm.at[faces[d][3]], dst_ref=hz.at[d],
+            send_sem=face_send.at[d], recv_sem=face_recv.at[d], device_id=faces[d][2],
+        )
 
     zero = jnp.zeros((block, LANES), jnp.float32)
 
@@ -159,69 +208,113 @@
             light = light + r2[p, k, 1]
         normal = image / (damping + light)
         nrm[p] = normal
-        rows[0, pl.ds(p, 1), :] = normal[strip - 1 :, :]
-        rows[1, pl.ds(p, 1), :] = normal[:1, :]
-
-    for p in range(depth):
+        rows[0, p] = normal[strip - 1 :, :]
+        rows[1, p] = normal[:1, :]
+        for d in range(2):
+            @pl.when(edges[d][0])
+            def _(d=d):
+                edge_copy(d, p).start()
+
+            if p == faces[d][3]:
+                @pl.when(faces[d][0])
+                def _(d=d):
+                    face_copy(d).start()
+
+    row = lax.broadcasted_iota(jnp.int32, (strip, width), 0)
+    column = lax.broadcasted_iota(jnp.int32, (strip, width), 1)
+
+    def lateral(p):
+        center = nrm[p]
+        before = jnp.where(row == 0, 0.0, pltpu.roll(center, 1, 0))
+        after = jnp.where(row == strip - 1, 0.0, pltpu.roll(center, strip - 1, 0))
+        left = jnp.where(column == 0, 0.0, pltpu.roll(center, 1, 1))
+        right = jnp.where(column == width - 1, 0.0, pltpu.roll(center, width - 1, 1))
+        return before + after + left + right - 6.0 * center
+
+    def wait_edges(p):
+        for d in range(2):
+            @pl.when(edges[d][1])
+            def _(d=d):
+                edge_copy(d, p).wait_recv()
+
+    def add_edges(p):
+        lap[p, pl.ds(0, 1), :] = lap[p, pl.ds(0, 1), :] + hx[0, p]
+        lap[p, pl.ds(strip - 1, 1), :] = lap[p, pl.ds(strip - 1, 1), :] + hx[1, p]
+
+    def emit(p):
+        pltpu.make_async_copy(lap.at[p], out.at[p], out_sem.at[p]).start()
+
+    for n, p in enumerate(order):
         pltpu.make_async_copy(rx.at[p], rx.at[p], rx_recv.at[p]).wait()
         expand(p)
         place(p, other)
         stage1(p)
         place(p, core)
-        if p >= 1:
-            stage2(p - 1)
-        if p >= 2:
-            finish(p - 2)
-    stage2(depth - 1)
+        if n >= 1:
+            stage2(order[n - 1])
+        if n >= 2:
+            finish(order[n - 2])
+    last = order[-1]
+    stage2(last)
     if depth >= 2:
-        finish(depth - 2)
-    finish(depth - 1)
-
-    halos = (
-        (shot < ns - 1, shot > 0, {"shot": lax.rem(shot + 1, ns)}, rows.at[0], hx.at[0], 0),
-        (shot > 0, shot < ns - 1, {"shot": lax.rem(shot + ns - 1, ns)}, rows.at[1], hx.at[1], 1),
-        (tile < nt - 1, tile > 0, {"tile": lax.rem(tile + 1, nt)}, nrm.at[depth - 1], hz.at[0], 2),
-        (tile > 0, tile < nt - 1, {"tile": lax.rem(tile + nt - 1, nt)}, nrm.at[0], hz.at[1], 3),
-    )
-
-    def halo_copy(item):
-        return pltpu.make_async_remote_copy(
-            src_ref=item[3], dst_ref=item[4], send_sem=h_send.at[item[5]], recv_sem=h_recv.at[item[5]], device_id=item[2]
-        )
-
-    for item in halos:
-        @pl.when(item[0])
-        def _(item=item):
-            halo_copy(item).start()
-
-        @pl.when(jnp.logical_not(item[1]))
-        def _(item=item):
-            item[4][...] = jnp.zeros(item[4].shape, jnp.float32)
-
-    for item in halos:
-        @pl.when(item[1])
-        def _(item=item):
-            halo_copy(item).wait_recv()
-
-    row = lax.broadcasted_iota(jnp.int32, (strip, width), 0)
-    column = lax.broadcasted_iota(jnp.int32, (strip, width), 1)
-    for p in range(depth):
-        center = nrm[p]
-        above = nrm[p - 1] if p > 0 else hz[0]
-        below = nrm[p + 1] if p < depth - 1 else hz[1]
-        beside = above + below
-        before = jnp.where(row == 0, hx[0, pl.ds(p, 1), :], pltpu.roll(center, 1, 0))
-        after = jnp.where(row == strip - 1, hx[1, pl.ds(p, 1), :], pltpu.roll(center, strip - 1, 0))
-        beside = beside + before + after
-        left = jnp.where(column == 0, 0.0, pltpu.roll(center, 1, 1))
-        right = jnp.where(column == width - 1, 0.0, pltpu.roll(center, width - 1, 1))
-        beside = beside + left + right
-        out[p] = beside - 6.0 * center
-
-    for item in halos:
-        @pl.when(item[0])
-        def _(item=item):
-            halo_copy(item).wait_send()
+        finish(order[-2])
+    early = order[:-1]
+    for d in range(2):
+        if faces[d][3] != last:
+            @pl.when(faces[d][1])
+            def _(d=d):
+                face_copy(d).wait_recv()
+    for p in early:
+        value = lateral(p)
+        for near, d in ((p - 1, 0), (p + 1, 1)):
+            if 0 <= near < depth:
+                if near != last:
+                    value = value + nrm[near]
+            elif faces[d][3] != last:
+                value = value + hz[d]
+        lap[p] = value
+        wait_edges(p)
+        add_edges(p)
+        if abs(p - last) > 1 and depth >= 3:
+            emit(p)
+    finish(last)
+    for p in early:
+        if abs(p - last) == 1:
+            lap[p] = lap[p] + nrm[last]
+            if depth >= 3:
+                emit(p)
+    value = lateral(last)
+    for near in (last - 1, last + 1):
+        if 0 <= near < depth:
+            value = value + nrm[near]
+    lap[last] = value
+    for d in range(2):
+        if faces[d][3] == last:
+            @pl.when(faces[d][1])
+            def _(d=d):
+                face_copy(d).wait_recv()
+
+    if depth < 3:
+        for d, p in ((0, 0), (1, depth - 1)):
+            if faces[d][3] == last or p == last:
+                lap[p] = lap[p] + hz[d]
+        for p in early:
+            emit(p)
+    wait_edges(last)
+    add_edges(last)
+    emit(last)
+    for p in order:
+        pltpu.make_async_copy(lap.at[p], out.at[p], out_sem.at[p]).wait()
+
+    for d in range(2):
+        @pl.when(edges[d][0])
+        def _(d=d):
+            for p in range(depth):
+                edge_copy(d, p).wait_send()
+
+        @pl.when(faces[d][0])
+        def _(d=d):
+            face_copy(d).wait_send()
 
     sent = cbuf.at[pl.ds(0, nt - 1)]
     pltpu.make_async_copy(sent, sent, c_send).wait()
@@ -248,8 +341,9 @@
             functools.partial(kernel, ns, nt),
             out_shape=jax.ShapeDtypeStruct((depth, strip, Y), f32),
             in_specs=[pl.BlockSpec(memory_space=pl.ANY)] * 3,
-            out_specs=pl.BlockSpec(memory_space=pltpu.VMEM),
+            out_specs=pl.BlockSpec(memory_space=pl.ANY),
             scratch_shapes=[
+                vmem((full_depth, 2, spd, samples, box_rows, box_cols), jnp.bfloat16),
                 vmem((depth, nt, 2, spd, samples, box_rows, box_cols), jnp.bfloat16),
                 vmem((nt, spd, 2), jnp.int32),
                 pltpu.SMEM((nt, spd, 2), jnp.int32),
@@ -258,9 +352,12 @@
                 vmem((depth, half_ns, 2, strip, Y), f32),
                 vmem((depth, half_ns - 1, 2, strip, Y), f32),
                 vmem((depth, strip, Y), f32),
-                vmem((2, depth, Y), f32),
+                vmem((2, depth, 1, Y), f32),
                 vmem((2, strip, Y), f32),
-                vmem((2, depth, Y), f32),
+                vmem((2, depth, 1, Y), f32),
+                vmem((depth, strip, Y), f32),
+                dma,
+                dma((depth,)),
                 dma((depth,)),
                 dma((depth,)),
                 dma,
@@ -270,8 +367,10 @@
                 dma((depth,)),
                 dma((depth,)),
                 dma((depth,)),
-                dma((4,)),
-                dma((4,)),
+                dma((2, depth)),
+                dma((2, depth)),
+                dma((2,)),
+                dma((2,)),
             ],
             compiler_params=pltpu.CompilerParams(
                 collective_id=0, has_side_effects=True, vmem_limit_bytes=60 * 1024 * 1024

time: 44.7 us -> 43.7 us (0.978)
  the two profiles are of different devices: /device:TPU:0 before, /device:TPU:1 now
where the time goes in v2:
time: 43.7 us; the launch traced here: 43.6 us
  Pallas kernels  41.9 us (96%)
  local copies, waits for them, and re-layouts  1.67 us (4%)
    pallas_call x1, Pallas kernels, step(): pl.pallas_call(functools.partial(kernel, ns, nt), out_shape=jax.ShapeDtyp...  41.9 us
    unnamed x1, local copies, waits for them, and re-layouts  1.67 us

profile of v2, /device:TPU:1, one launch (start us, length us, event | category | flops | bytes accessed | tf_op | source)
XLA Modules:
  0.0 43.6 jit_solution(10240718609345289949)
XLA Ops:
  0.0 41.9 %shard_map.37 = f32[4,64,256]{2,1,0:T(8,128)} custom-call(bf16[2,1,32,32,128]{4,3,2,1,0:T(8,128)(2,1)} %src.1, bf16[2,1,32,32,128]{4,3,2,1,0:T(8,128)(2,1)} %rcv.1, s32[2,2]{1,0:T(2,128)} %cor.1), custom_call_target="tpu_custom_call" | custom-call | tf_op jit(solution)/shard_map/pallas_call | solution.py:340
  41.9 1.7 %copy.5 = f32[4,64,256]{2,1,0:T(8,128)} copy(f32[4,64,256]{2,1,0:T(8,128)} %shard_map.37) | data formatting | bytes 524288

commit v3 on v2

--- a/solution.py
+++ b/solution.py
@@ -35,7 +35,7 @@
 def kernel(
     ns, nt, src, rcv, cor, out, sbuf, rx, cbuf, csm, boxes, acc, r1, r2, nrm, hx, hz, rows, lap,
     in_sem, out_sem, rx_send, rx_recv, c_send, c_recv, c_local,
-    s1_send, s1_recv, s2_send, s2_recv, row_send, row_recv, face_send, face_recv,
+    s1_send, s1_recv, s2_send, s2_recv, row_send, row_recv, face_send, face_recv, token,
 ):
     depth, strip, width = nrm.shape
     spd, samples = src.shape[0], src.shape[1]
@@ -55,8 +55,20 @@
     barrier = pltpu.get_barrier_semaphore()
     for k in range(1, ns):
         pl.semaphore_signal(barrier, inc=1, device_id={"shot": lax.rem(shot + k, ns)})
-    for k in range(1, nt):
-        pl.semaphore_signal(barrier, inc=1, device_id={"tile": lax.rem(tile + k, nt)})
+    place_at, side = tile // 2, lax.rem(tile, 2)
+    places = nt // 2
+    has_next, has_last = place_at < places - 1, place_at > 0
+    after_me, before_me = lax.rem(tile + 2, nt), lax.rem(tile + nt - 2, nt)
+    beside_me = tile + 1 - 2 * side
+    pl.semaphore_signal(barrier, inc=1, device_id={"tile": beside_me})
+
+    @pl.when(has_next)
+    def _():
+        pl.semaphore_signal(barrier, inc=1, device_id={"tile": after_me})
+
+    @pl.when(has_last)
+    def _():
+        pl.semaphore_signal(barrier, inc=1, device_id={"tile": before_me})
 
     for w, ref in enumerate((src, rcv)):
         for i in range(spd):
@@ -68,22 +80,83 @@
             pltpu.make_async_copy(ref.at[:, :, tile * depth + p], rx.at[p, tile, w], rx_recv.at[p]).start()
     pltpu.make_async_copy(sbuf, sbuf, in_sem).wait()
 
-    pl.semaphore_wait(barrier, ns - 1 + nt - 1)
+    zero = jnp.zeros((block, LANES), jnp.float32)
+
+    def clear(s, carry):
+        for q in range(2):
+            for h in range(halves):
+                boxes[s, q, h, pl.ds(0, block), :] = zero
+                boxes[s, q, h, pl.ds(block + box_rows, block), :] = zero
+        return carry
+
+    lax.fori_loop(0, shots, clear, 0)
+
+    pl.semaphore_wait(barrier, ns + jnp.minimum(place_at, 1) + jnp.minimum(places - 1 - place_at, 1))
+
+    @pl.when(has_last)
+    def _():
+        pl.semaphore_signal(token.at[0, 1], inc=1, device_id={"tile": before_me})
+
+    @pl.when(has_next)
+    def _():
+        pl.semaphore_signal(token.at[1, 1], inc=1, device_id={"tile": after_me})
+
+    def send_corner(to):
+        pltpu.make_async_remote_copy(
+            src_ref=cor, dst_ref=cbuf.at[tile], send_sem=c_send, recv_sem=c_recv, device_id={"tile": to}
+        ).start()
+
+    def send_plane(p, to):
+        pltpu.make_async_remote_copy(
+            src_ref=sbuf.at[to * depth + p],
+            dst_ref=rx.at[p, tile],
+            send_sem=rx_send.at[p],
+            recv_sem=rx_recv.at[p],
+            device_id={"tile": to},
+        ).start()
+
+    def send_all(to):
+        send_corner(to)
+        for p in order:
+            send_plane(p, to)
+
+    @pl.when(has_next)
+    def _():
+        send_all(after_me)
+
+    @pl.when(has_last)
+    def _():
+        send_all(before_me)
+
+    send_all(beside_me)
+
+    for r in range(1, places):
+        @pl.when(place_at + r < places)
+        def _(r=r):
+            pl.semaphore_wait(token.at[0, r], 1)
+
+            @pl.when(has_last)
+            def _():
+                pl.semaphore_signal(token.at[0, r + 1], inc=1, device_id={"tile": before_me})
+
+        @pl.when(place_at >= r)
+        def _(r=r):
+            pl.semaphore_wait(token.at[1, r], 1)
+
+            @pl.when(has_next)
+            def _():
+                pl.semaphore_signal(token.at[1, r + 1], inc=1, device_id={"tile": after_me})
 
     for p in order:
         for k in range(nt - 1, 0, -1):
             to = partner(tile, k, nt)
-            if p == order[0]:
-                pltpu.make_async_remote_copy(
-                    src_ref=cor, dst_ref=cbuf.at[tile], send_sem=c_send, recv_sem=c_recv, device_id={"tile": to}
-                ).start()
-            pltpu.make_async_remote_copy(
-                src_ref=sbuf.at[to * depth + p],
-                dst_ref=rx.at[p, tile],
-                send_sem=rx_send.at[p],
-                recv_sem=rx_recv.at[p],
-                device_id={"tile": to},
-            ).start()
+            near = (to == beside_me) | ((to == after_me) & has_next) | ((to == before_me) & has_last)
+
+            @pl.when(jnp.logical_not(near))
+            def _(p=p, to=to):
+                if p == order[0]:
+                    send_corner(to)
+                send_plane(p, to)
 
     edges = (
         (shot < ns - 1, shot > 0, {"shot": lax.rem(shot + 1, ns)}),
@@ -113,17 +186,6 @@
             src_ref=nrm.at[faces[d][3]], dst_ref=hz.at[d],
             send_sem=face_send.at[d], recv_sem=face_recv.at[d], device_id=faces[d][2],
         )
-
-    zero = jnp.zeros((block, LANES), jnp.float32)
-
-    def clear(s, carry):
-        for q in range(2):
-            for h in range(halves):
-                boxes[s, q, h, pl.ds(0, block), :] = zero
-                boxes[s, q, h, pl.ds(block + box_rows, block), :] = zero
-        return carry
-
-    lax.fori_loop(0, shots, clear, 0)
 
     pltpu.make_async_copy(cbuf, cbuf, c_recv).wait()
     to_scalar = pltpu.make_async_copy(cbuf, csm, c_local)
@@ -371,6 +433,7 @@
                 dma((2, depth)),
                 dma((2,)),
                 dma((2,)),
+                pltpu.SemaphoreType.REGULAR((2, nt // 2 + 1)),
             ],
             compiler_params=pltpu.CompilerParams(
                 collective_id=0, has_side_effects=True, vmem_limit_bytes=60 * 1024 * 1024

time: 43.7 us -> 45.9 us (1.050)
  Pallas kernels: 41.9 us -> 44.1 us
    pallas_call x1, Pallas kernels: 41.9 us -> 44.1 us  [step(): pl.pallas_call(functools.partial(kernel, ns, nt), out_shape=jax.ShapeDtyp...]
where the time goes in v3:
time: 45.9 us; the launch traced here: 45.8 us
  Pallas kernels  44.1 us (96%)
  local copies, waits for them, and re-layouts  1.67 us (4%)
    pallas_call x1, Pallas kernels, step(): pl.pallas_call(functools.partial(kernel, ns, nt), out_shape=jax.ShapeDtyp...  44.1 us
    unnamed x1, local copies, waits for them, and re-layouts  1.67 us

profile of v3, /device:TPU:1, one launch (start us, length us, event | category | flops | bytes accessed | tf_op | source)
XLA Modules:
  0.0 45.8 jit_solution(5341075526267486673)
XLA Ops:
  0.0 44.1 %shard_map.37 = f32[4,64,256]{2,1,0:T(8,128)} custom-call(bf16[2,1,32,32,128]{4,3,2,1,0:T(8,128)(2,1)} %src.1, bf16[2,1,32,32,128]{4,3,2,1,0:T(8,128)(2,1)} %rcv.1, s32[2,2]{1,0:T(2,128)} %cor.1), custom_call_target="tpu_custom_call" | custom-call | tf_op jit(solution)/shard_map/pallas_call | solution.py:402
  44.1 1.7 %copy.5 = f32[4,64,256]{2,1,0:T(8,128)} copy(f32[4,64,256]{2,1,0:T(8,128)} %shard_map.37) | data formatting | bytes 524288

commit v4 on v3

--- a/solution.py
+++ b/solution.py
@@ -117,8 +117,7 @@
 
     def send_all(to):
         send_corner(to)
-        for p in order:
-            send_plane(p, to)
+        send_plane(order[0], to)
 
     @pl.when(has_next)
     def _():
@@ -152,10 +151,12 @@
             to = partner(tile, k, nt)
             near = (to == beside_me) | ((to == after_me) & has_next) | ((to == before_me) & has_last)
 
-            @pl.when(jnp.logical_not(near))
-            def _(p=p, to=to):
-                if p == order[0]:
+            if p == order[0]:
+                @pl.when(jnp.logical_not(near))
+                def _(p=p, to=to):
                     send_corner(to)
+                    send_plane(p, to)
+            else:
                 send_plane(p, to)
 
     edges = (

time: 45.9 us -> 45.4 us (0.989)
  Pallas kernels: 44.1 us -> 43.5 us
    pallas_call x1, Pallas kernels: 44.1 us -> 43.5 us  [step(): pl.pallas_call(functools.partial(kernel, ns, nt), out_shape=jax.ShapeDtyp...]
where the time goes in v4:
time: 45.4 us; the launch traced here: 45.2 us
  Pallas kernels  43.5 us (96%)
  local copies, waits for them, and re-layouts  1.67 us (4%)
    pallas_call x1, Pallas kernels, step(): pl.pallas_call(functools.partial(kernel, ns, nt), out_shape=jax.ShapeDtyp...  43.5 us
    unnamed x1, local copies, waits for them, and re-layouts  1.67 us

profile of v4, /device:TPU:1, one launch (start us, length us, event | category | flops | bytes accessed | tf_op | source)
XLA Modules:
  0.0 45.2 jit_solution(13820250406895290042)
XLA Ops:
  0.0 43.5 %shard_map.37 = f32[4,64,256]{2,1,0:T(8,128)} custom-call(bf16[2,1,32,32,128]{4,3,2,1,0:T(8,128)(2,1)} %src.1, bf16[2,1,32,32,128]{4,3,2,1,0:T(8,128)(2,1)} %rcv.1, s32[2,2]{1,0:T(2,128)} %cor.1), custom_call_target="tpu_custom_call" | custom-call | tf_op jit(solution)/shard_map/pallas_call | solution.py:403
  43.5 1.7 %copy.5 = f32[4,64,256]{2,1,0:T(8,128)} copy(f32[4,64,256]{2,1,0:T(8,128)} %shard_map.37) | data formatting | bytes 524288
